TPU v7x, 32 devices: a whole 2x2x4 slice. The times are simulated.
32 devices in a mesh: leaf: 8 (over z, y), grid: 4 (over x, core).
Axes of the slice: x: 2, y: 2, z: 4, core: 2. Of those that a mesh axis runs over, the one named last changes fastest.
Arguments:
- source_leaf: float32 [8, 4096], P(None, ('leaf', 'grid')), may hold values from -6 to 6
- block_leaf: float32 [4096, 128], P(('leaf', 'grid')), may hold values from -0.5 to 0.5
- expand_leaf: float32 [4096, 128], P(('leaf', 'grid')), may hold values from -0.5 to 0.5
- basis_leaf: float32 [4096, 256], P(('leaf', 'grid')), may hold values from -0.25 to 0.25
- pivot_leaf: float32 [4096], P(('leaf', 'grid')), may hold values from -2 to 2
- couple_leaf: float32 [8192, 128], P(('leaf', 'grid')), may hold values from -0.5 to 0.5
- ranks_leaf: int32 [8, 2], replicated, may hold values from 32 to 128
- targets_leaf: int32 [8192], P(('leaf', 'grid')), may hold values from 0 to 2047, as said below
- source_middle: float32 [8, 4096], P(None, ('leaf', 'grid')), may hold values from -6 to 6
- block_middle: float32 [4096, 128], P(('leaf', 'grid')), may hold values from -0.5 to 0.5
- expand_middle: float32 [4096, 128], P(('leaf', 'grid')), may hold values from -0.5 to 0.5
- basis_middle: float32 [4096, 256], P(('leaf', 'grid')), may hold values from -0.1875 to 0.1875
- pivot_middle: float32 [4096], P(('leaf', 'grid')), may hold values from -2 to 2
- couple_middle: float32 [4096, 128], P(('leaf', 'grid')), may hold values from -0.5 to 0.5
- ranks_middle: int32 [4, 2], replicated, may hold values from 32 to 128
- targets_middle: int32 [4096], P(('leaf', 'grid')), may hold values from 0 to 4095, as said below
- source_upper: float32 [8, 4096], P(None, ('leaf', 'grid')), may hold values from -6 to 6
- block_upper: float32 [4096, 128], P(('leaf', 'grid')), may hold values from -0.5 to 0.5
- expand_upper: float32 [4096, 128], P(('leaf', 'grid')), may hold values from -0.5 to 0.5
- basis_upper: float32 [4096, 256], P(('leaf', 'grid')), may hold values from -0.125 to 0.125
- pivot_upper: float32 [4096], P(('leaf', 'grid')), may hold values from -2 to 2
- couple_upper: float32 [4096, 128], P(('leaf', 'grid')), may hold values from -0.5 to 0.5
- ranks_upper: int32 [2, 2], replicated, may hold values from 32 to 128
- targets_upper: int32 [4096], P(('leaf', 'grid')), may hold values from 0 to 4095, as said below
- source_root: float32 [8, 4096], P(None, ('leaf', 'grid')), may hold values from -6 to 6
- block_root: float32 [4096, 128], P(('leaf', 'grid')), may hold values from -0.5 to 0.5
- expand_root: float32 [4096, 128], P(('leaf', 'grid')), may hold values from -0.5 to 0.5
- basis_root: float32 [4096, 256], P(('leaf', 'grid')), may hold values from -0.09375 to 0.09375
- pivot_root: float32 [4096], P(('leaf', 'grid')), may hold values from -2 to 2
- ranks_root: int32 [1, 2], replicated, may hold values from 32 to 128
Outputs:
- answer_leaf: float32 [8, 4096], P(None, ('leaf', 'grid'))
- answer_middle: float32 [8, 4096], P(None, ('leaf', 'grid'))
- answer_upper: float32 [8, 4096], P(None, ('leaf', 'grid'))
- answer_root: float32 [8, 4096], P(None, ('leaf', 'grid'))
Inputs may be any that keep to these rules, and one draw needn't show every extreme that they name: `targets_leaf`: within one leaf front the 1024 entries are distinct; each names a row of the parent front's row vector of 2048 rows. Split that vector's separator part and its update part each evenly, in order, over the parent's devices (leaf then grid); then the rows of one device name at most 32 rows held by any one of them, and exactly that many for some. `targets_middle`: within one middle front the entries are distinct; each names a row of the parent front's row vector of 4096 rows. Split likewise over the parent's devices, the rows of one device name at most 8 rows held by any one of them, and exactly that many for some. `targets_upper`: within one upper front the entries are distinct; each names a row of the root separator. Split evenly in order over all devices, the rows of one device name at most 4 rows held by any one of them, and exactly that many for some.
All inputs are finite; a program needn't handle non-finite values.
Results may differ from a plain program's by a relative error of at most 0.0003.
Values sent between devices are 32-bit elements; how exact they have to be, the bound alone decides.
A program may use at most 128 MiB of HBM per device.

v0:
```python
import jax
import jax.numpy as jnp
from jax import lax
from jax.sharding import PartitionSpec as P

BLOCK = 128
RANK = 128
HIGH_PRECISION = lax.Precision.HIGHEST


def from_partner(value, axis, distance):
    mask = 2**distance
    pairs = [(source, source ^ mask) for source in range(lax.axis_size(axis))]
    return lax.ppermute(value, axis, pairs)


def mult(left, right):
    return jnp.dot(left, right, precision=HIGH_PRECISION, preferred_element_type=jnp.float32)


def inner(left, right):
    return lax.dot_general(
        left,
        right,
        (((0,), (0,)), ((), ())),
        precision=HIGH_PRECISION,
        preferred_element_type=jnp.float32,
    )


def outer(left, right):
    return lax.dot_general(
        left,
        right,
        (((1,), (1,)), ((), ())),
        precision=HIGH_PRECISION,
        preferred_element_type=jnp.float32,
    )


def paired_total(partial_value, bits):
    summed = lax.psum(partial_value, "grid")
    for bit in range(bits):
        summed = summed + from_partner(summed, "leaf", bit)
    return summed


def group_total(partial_value, bits):
    return paired_total(partial_value, bits)


def upper_bit(place, bit):
    return place // (1 << bit) % 2 == 1


def group_extend(stack, bits, place):
    for bit in reversed(range(bits)):
        half = stack.shape[2] // 2
        lower_part = stack[:, :, :half]
        upper_part = stack[:, :, half:]
        flag = upper_bit(place, bit)
        keep = jnp.where(flag, upper_part, lower_part)
        send = jnp.where(flag, lower_part, upper_part)
        stack = keep + from_partner(send, "leaf", bit)
    return lax.psum_scatter(stack, "grid", scatter_dimension=2, tiled=True)


def group_fetch(stack, bits, place):
    current = lax.all_gather(stack, "grid", axis=2, tiled=True)
    for bit in range(bits):
        other = from_partner(current, "leaf", bit)
        flag = upper_bit(place, bit)
        current = jnp.where(
            flag,
            jnp.concatenate([other, current], axis=2),
            jnp.concatenate([current, other], axis=2),
        )
    return current


def forward_level(source, incoming, block, expand, basis, pivot, ranks, bits, front):
    level_batch_index = source if incoming is None else source + incoming
    count, width = level_batch_index.shape
    tiles = block.reshape(width // BLOCK, BLOCK, BLOCK)
    local_portion = jnp.einsum(
        "anh,nhk->ank",
        level_batch_index.reshape(count, width // BLOCK, BLOCK),
        tiles,
        precision=HIGH_PRECISION,
    ).reshape(count, width)
    query_lookup = basis[:, :RANK]
    coupling_right_factor = basis[:, RANK:]
    rank_pair = lax.dynamic_index_in_dim(ranks, front, 0, keepdims=False)
    columns = jnp.arange(RANK, dtype=jnp.int32)
    head_mask_grid = (columns < rank_pair[0]).astype(jnp.float32)
    column_mask_grid = (columns < rank_pair[1]).astype(jnp.float32)
    partial_value = jnp.concatenate(
        [
            mult(level_batch_index, query_lookup),
            mult(local_portion, coupling_right_factor),
            inner(expand, coupling_right_factor),
        ],
        axis=0,
    )
    total = group_total(partial_value, bits)
    hidden_q = total[:count] * head_mask_grid
    cross = total[2 * count :]
    intermediate_entries = local_portion + outer(hidden_q, expand)
    weight_entries = (total[count : 2 * count] + mult(hidden_q, cross)) * column_mask_grid
    return (
        intermediate_entries * pivot[None, :],
        weight_entries,
        (tiles, query_lookup, coupling_right_factor, cross, head_mask_grid, column_mask_grid),
    )


def backward_level(correction_entries, x_upd, couple, expand, parts, bits):
    tiles, query_lookup, coupling_right_factor, cross, head_mask_grid, column_mask_grid = parts
    count, width = correction_entries.shape
    if x_upd is None:
        total = group_total(mult(correction_entries, expand), bits)
        remainder_rows = correction_entries
        right_projection = total * head_mask_grid
    else:
        total = group_total(
            jnp.concatenate([mult(x_upd, couple), mult(correction_entries, expand)], axis=0), bits
        )
        solve_direction = total[:count] * column_mask_grid
        remainder_rows = correction_entries - outer(solve_direction, coupling_right_factor)
        right_projection = (total[count:] - outer(solve_direction, cross)) * head_mask_grid
    local_portion = jnp.einsum(
        "anh,nkh->ank",
        remainder_rows.reshape(count, width // BLOCK, BLOCK),
        tiles,
        precision=HIGH_PRECISION,
    ).reshape(count, width)
    return local_portion + outer(right_projection, query_lookup)


def extend(update, targets, sep_total, has_update, bits, place):
    count = update.shape[0]
    pieces = 2 if has_update else 1
    rows = sep_total * pieces
    buffer = jnp.zeros((count, rows), jnp.float32).at[:, targets].add(update)
    if has_update:
        stack = jnp.stack([buffer[:, :sep_total], buffer[:, sep_total:]])
    else:
        stack = buffer[None]
    return group_extend(stack, bits, place)


def fetch(stack, targets, bits, place):
    front_full = group_fetch(stack, bits, place)
    rows = front_full.transpose(1, 0, 2).reshape(front_full.shape[1], -1)
    return jnp.take(rows, targets, axis=1)


def shards(
    source_leaf,
    block_leaf,
    expand_leaf,
    basis_leaf,
    pivot_leaf,
    couple_leaf,
    ranks_leaf,
    targets_leaf,
    source_middle,
    block_middle,
    expand_middle,
    basis_middle,
    pivot_middle,
    couple_middle,
    ranks_middle,
    targets_middle,
    source_upper,
    block_upper,
    expand_upper,
    basis_upper,
    pivot_upper,
    couple_upper,
    ranks_upper,
    targets_upper,
    source_root,
    block_root,
    expand_root,
    basis_root,
    pivot_root,
    ranks_root,
):
    levels = [
        (
            source_leaf,
            block_leaf,
            expand_leaf,
            basis_leaf,
            pivot_leaf,
            couple_leaf,
            ranks_leaf,
            targets_leaf,
        ),
        (
            source_middle,
            block_middle,
            expand_middle,
            basis_middle,
            pivot_middle,
            couple_middle,
            ranks_middle,
            targets_middle,
        ),
        (
            source_upper,
            block_upper,
            expand_upper,
            basis_upper,
            pivot_upper,
            couple_upper,
            ranks_upper,
            targets_upper,
        ),
        (source_root, block_root, expand_root, basis_root, pivot_root, None, ranks_root, None),
    ]
    leaves = lax.axis_size("leaf")
    across = lax.axis_size("grid")
    place = lax.axis_index("leaf")
    depth = leaves.bit_length() - 1
    groups = [1, leaves // 4, leaves // 2, leaves]
    bit_counts = [0, depth - 2, depth - 1, depth]
    owners = [place // groups[level] for level in range(4)]
    inc_sep = None
    inc_upd = None
    saved = []
    for level in range(4):
        source, block, expand, basis, pivot, couple, ranks, targets = levels[level]
        correction_entries, weight_entries, parts = forward_level(
            source, inc_sep, block, expand, basis, pivot, ranks, bit_counts[level], owners[level]
        )
        saved.append((correction_entries, parts))
        if level < 3:
            update = -outer(weight_entries, couple)
            if inc_upd is not None:
                update = update + inc_upd
            sep_total = levels[level + 1][0].shape[1] * across * groups[level + 1]
            has_update = level + 1 < 3
            stack = extend(update, targets, sep_total, has_update, bit_counts[level + 1], place)
            inc_sep = stack[0]
            inc_upd = stack[1] if has_update else None
    answers = [None, None, None, None]
    parent_stack = None
    for level in (3, 2, 1, 0):
        correction_entries, parts = saved[level]
        couple = levels[level][5]
        expand = levels[level][2]
        targets = levels[level][7]
        x_upd = None
        if level < 3:
            x_upd = fetch(parent_stack, targets, bit_counts[level + 1], place)
        xvals = backward_level(correction_entries, x_upd, couple, expand, parts, bit_counts[level])
        answers[level] = xvals
        if level > 0:
            parent_stack = xvals[None] if x_upd is None else jnp.stack([xvals, x_upd])
    return (answers[0], answers[1], answers[2], answers[3])


def solution(mesh):
    in_specs = (
        P(None, ("leaf", "grid")),
        P(("leaf", "grid"), None),
        P(("leaf", "grid"), None),
        P(("leaf", "grid"), None),
        P(("leaf", "grid")),
        P(("leaf", "grid"), None),
        P(),
        P(("leaf", "grid")),
        P(None, ("leaf", "grid")),
        P(("leaf", "grid"), None),
        P(("leaf", "grid"), None),
        P(("leaf", "grid"), None),
        P(("leaf", "grid")),
        P(("leaf", "grid"), None),
        P(),
        P(("leaf", "grid")),
        P(None, ("leaf", "grid")),
        P(("leaf", "grid"), None),
        P(("leaf", "grid"), None),
        P(("leaf", "grid"), None),
        P(("leaf", "grid")),
        P(("leaf", "grid"), None),
        P(),
        P(("leaf", "grid")),
        P(None, ("leaf", "grid")),
        P(("leaf", "grid"), None),
        P(("leaf", "grid"), None),
        P(("leaf", "grid"), None),
        P(("leaf", "grid")),
        P(),
    )
    out_specs = (
        P(None, ("leaf", "grid")),
        P(None, ("leaf", "grid")),
        P(None, ("leaf", "grid")),
        P(None, ("leaf", "grid")),
    )
    return jax.shard_map(shards, mesh=mesh, in_specs=in_specs, out_specs=out_specs, check_vma=False)
```

profile of v0, /device:TPU:0, one launch (start us, length us, event | category | flops | bytes accessed | tf_op | source)
XLA Modules:
  0.0 397.3 jit_solution(7661426514770940477)
XLA Ops:
  17.3 27.4 %all-reduce.5.cloned.1.call-done = f32[144,128]{1,0:T(8,128)} async-done(((f32[144,128]{1,0:T(8,128)}), f32[144,128]{1,0:T(8,128)}) %all-reduce.5.cloned.1.call-update) | async-done | bytes 73744 | tf_op jit(solution)/shard_map/psum | solution.py:42
  53.4 21.0 %reduce-scatter.4.cloned.1.call-done = f32[2,8,128]{2,1,0:T(8,128)} async-done(((f32[2,8,512]{2,1,0:T(8,128)}), f32[2,8,128]{2,1,0:T(8,128)}) %reduce-scatter.4.cloned.1.call-update) | async-done | bytes 8208 | tf_op jit(solution)/shard_map/reduce_scatter | solution.py:65
  77.7 29.1 %all-reduce.7.cloned.1.call-done = f32[144,128]{1,0:T(8,128)} async-done(((f32[144,128]{1,0:T(8,128)}), f32[144,128]{1,0:T(8,128)}) %all-reduce.7.cloned.1.call-update) | async-done | bytes 73744 | tf_op jit(solution)/shard_map/psum | solution.py:42
  128.0 21.2 %reduce-scatter.6.cloned.1.call-done = f32[2,8,128]{2,1,0:T(8,128)} async-done(((f32[2,8,512]{2,1,0:T(8,128)}), f32[2,8,128]{2,1,0:T(8,128)}) %reduce-scatter.6.cloned.1.call-update) | async-done | bytes 8208 | tf_op jit(solution)/shard_map/reduce_scatter | solution.py:65
  152.4 29.2 %all-reduce.9.cloned.1.call-done = f32[144,128]{1,0:T(8,128)} async-done(((f32[144,128]{1,0:T(8,128)}), f32[144,128]{1,0:T(8,128)}) %all-reduce.9.cloned.1.call-update) | async-done | bytes 73744 | tf_op jit(solution)/shard_map/psum | solution.py:42
  196.0 2.7 collective-permute-start.6
  198.7 2.8 collective-permute-done.6
  205.2 9.0 %collective-permute-done.7 = f32[1,8,1024]{1,2,0:T(8,128)S(1)} collective-permute-done((f32[1,8,1024]{1,2,0:T(8,128)S(1)}, f32[1,8,1024]{1,2,0:T(8,128)S(1)}, u32[]{:S(2)}, u32[]{:S(2)}) %collective-permute-start.7) | collective-permute-done | bytes 32800 | tf_op jit(solution)/shard_map/ppermute | solution.py:14
  216.7 4.2 %collective-permute-done.8 = f32[1,8,512]{1,2,0:T(8,128)S(1)} collective-permute-done((f32[1,8,512]{1,2,0:T(8,128)S(1)}, f32[1,8,512]{1,2,0:T(8,128)S(1)}, u32[]{:S(2)}, u32[]{:S(2)}) %collective-permute-start.8) | collective-permute-done | bytes 16416 | tf_op jit(solution)/shard_map/ppermute | solution.py:14
  222.3 20.4 %reduce-scatter.8.cloned.1.call-done = f32[1,8,128]{1,2,0:T(8,128)} async-done(((f32[1,8,512]{1,2,0:T(8,128)}), f32[1,8,128]{1,2,0:T(8,128)}) %reduce-scatter.8.cloned.1.call-update) | async-done | bytes 4112 | tf_op jit(solution)/shard_map/reduce_scatter | solution.py:65
  246.3 29.2 %all-reduce.11.cloned.1.call-done = f32[144,128]{1,0:T(8,128)} async-done(((f32[144,128]{1,0:T(8,128)}), f32[144,128]{1,0:T(8,128)}) %all-reduce.11.cloned.1.call-update) | async-done | bytes 73744 | tf_op jit(solution)/shard_map/psum | solution.py:42
  277.4 3.0 collective-permute-done.9
  283.1 2.6 collective-permute-done.10
  285.7 2.7 collective-permute-start.11
  288.5 2.5 collective-permute-done.11
  291.4 5.9 %psum.60 = f32[8,128]{1,0:T(8,128)S(1)} all-reduce(f32[8,128]{1,0:T(8,128)S(1)} %fusion.123), channel_id=1, replica_groups=mesh['leaf'=8,'grid'=4] {'grid'}, use_global_device_ids=true, to_apply=%region_10.11 | all-reduce | flops 1024 | bytes 8192 | tf_op jit(solution)/shard_map/psum | solution.py:42
  304.6 3.0 collective-permute-start.14
  309.4 5.6 %all-gather = f32[8,512]{1,0:T(8,128)S(1)} all-gather(f32[8,128]{1,0:T(8,128)S(1)} %convolution_add_fusion.3), channel_id=2, replica_groups=mesh['leaf'=8,'grid'=4] {'grid'}, dimensions={1}, use_global_device_ids=true | all-gather | bytes 20480 | tf_op jit(solution)/shard_map/all_gather | solution.py:69
  322.6 3.0 collective-permute-start.17
  330.0 5.8 %psum.61 = f32[16,128]{1,0:T(8,128)S(1)} all-reduce(f32[16,128]{1,0:T(8,128)S(1)} %pad_maximum_fusion.6), channel_id=1, replica_groups=mesh['leaf'=8,'grid'=4] {'grid'}, use_global_device_ids=true, to_apply=%region_11.13 | all-reduce | flops 2048 | bytes 16384 | tf_op jit(solution)/shard_map/psum | solution.py:42
  346.0 5.5 %all_gather.10 = f32[2,8,512]{2,1,0:T(8,128)S(1)} all-gather(f32[2,8,128]{2,1,0:T(8,128)S(1)} %pad_maximum_fusion.7), channel_id=1, replica_groups=mesh['leaf'=8,'grid'=4] {'grid'}, dimensions={2}, use_global_device_ids=true | all-gather | bytes 40960 | tf_op jit(solution)/shard_map/all_gather | solution.py:69
  361.3 5.8 %psum.62 = f32[16,128]{1,0:T(8,128)S(1)} all-reduce(f32[16,128]{1,0:T(8,128)S(1)} %pad_maximum_fusion.8), channel_id=1, replica_groups=mesh['leaf'=8,'grid'=4] {'grid'}, use_global_device_ids=true, to_apply=%region_12.14 | all-reduce | flops 2048 | bytes 16384 | tf_op jit(solution)/shard_map/psum | solution.py:42
  371.7 5.3 %all_gather.11 = f32[2,8,512]{2,1,0:T(8,128)S(1)} all-gather(f32[2,8,128]{2,1,0:T(8,128)S(1)} %pad_maximum_fusion.9), channel_id=1, replica_groups=mesh['leaf'=8,'grid'=4] {'grid'}, dimensions={2}, use_global_device_ids=true | all-gather | bytes 40960 | tf_op jit(solution)/shard_map/all_gather | solution.py:69
  382.4 6.5 %psum.63 = f32[16,128]{1,0:T(8,128)S(1)} all-reduce(f32[16,128]{1,0:T(8,128)S(1)} %pad_maximum_fusion.10), channel_id=1, replica_groups=mesh['leaf'=8,'grid'=4] {'grid'}, use_global_device_ids=true, to_apply=%region_13.15 | all-reduce | flops 2048 | bytes 16384 | tf_op jit(solution)/shard_map/psum | solution.py:42
  (304 shorter events, 128.9 us)
Async XLA Ops:
  7.2 37.5 %all-reduce.5.cloned.1.call-start = ((), (), s32[]{:S(2)}) async-start(), calls=%async_computation.3 | async-start | bytes 147456 | tf_op jit(solution)/shard_map/psum | solution.py:42
  12.1 62.3 %reduce-scatter.4.cloned.1.call-start = ((), (), s32[]{:S(2)}) async-start(), calls=%async_computation.4 | async-start | bytes 40960 | tf_op jit(solution)/shard_map/reduce_scatter | solution.py:65
  48.2 4.0 collective-permute-start
  52.8 54.0 %all-reduce.7.cloned.1.call-start = ((), (), s32[]{:S(2)}) async-start(), calls=%async_computation.5 | async-start | bytes 147456 | tf_op jit(solution)/shard_map/psum | solution.py:42
  77.0 72.3 %reduce-scatter.6.cloned.1.call-start = ((), (), s32[]{:S(2)}) async-start(), calls=%async_computation.6 | async-start | bytes 40960 | tf_op jit(solution)/shard_map/reduce_scatter | solution.py:65
  106.8 4.9 %collective-permute-start.1 = (f32[144,128]{1,0:T(8,128)}, f32[144,128]{1,0:T(8,128)S(1)}, u32[]{:S(2)}, u32[]{:S(2)}) collective-permute-start(f32[144,128]{1,0:T(8,128)} %all-reduce.7.cloned.1.call-done), channel_id=1, source_target_pairs={{0,4},{4,0},{8,12},{12,8},{16,20},{20,16},{24,28},{28,24},{1,5},{5... | collective-permute-start | bytes 221192 | tf_op jit(solution)/shard_map/ppermute | solution.py:14
  118.9 4.3 %collective-permute-start.2 = (f32[2,8,1024]{2,1,0:T(8,128)S(1)}, f32[2,8,1024]{2,1,0:T(8,128)S(1)}, u32[]{:S(2)}, u32[]{:S(2)}) collective-permute-start(f32[2,8,1024]{2,1,0:T(8,128)S(1)} %broadcast_select_fusion), channel_id=1, source_target_pairs={{0,8},{4,12},{8,0},{12,4},{16,24},{20,28},{24,16},{28,20},{1,9},{5... | collective-permute-start | bytes 196616 | tf_op jit(solution)/shard_map/ppermute | solution.py:14
  123.3 4.0 %collective-permute-start.3 = (f32[2,8,512]{2,1,0:T(8,128)S(1)}, f32[2,8,512]{2,1,0:T(8,128)S(1)}, u32[]{:S(2)}, u32[]{:S(2)}) collective-permute-start(f32[2,8,512]{2,1,0:T(8,128)S(1)} %slice_select_fusion.3), channel_id=1, source_target_pairs={{0,4},{4,0},{8,12},{12,8},{16,20},{20,16},{24,28},{28,24},{1,5},{5... | collective-permute-start | bytes 98312 | tf_op jit(solution)/shard_map/ppermute | solution.py:14
  127.9 53.7 %all-reduce.9.cloned.1.call-start = ((), (), s32[]{:S(2)}) async-start(), calls=%async_computation.7 | async-start | bytes 147456 | tf_op jit(solution)/shard_map/psum | solution.py:42
  151.8 90.8 %reduce-scatter.8.cloned.1.call-start = ((), (), s32[]{:S(2)}) async-start(), calls=%async_computation.8 | async-start | bytes 327680 | tf_op jit(solution)/shard_map/reduce_scatter | solution.py:65
  181.6 4.9 %collective-permute-start.4 = (f32[144,128]{1,0:T(8,128)}, f32[144,128]{1,0:T(8,128)S(1)}, u32[]{:S(2)}, u32[]{:S(2)}) collective-permute-start(f32[144,128]{1,0:T(8,128)} %all-reduce.9.cloned.1.call-done), channel_id=1, source_target_pairs={{0,4},{4,0},{8,12},{12,8},{16,20},{20,16},{24,28},{28,24},{1,5},{5... | collective-permute-start | bytes 221192 | tf_op jit(solution)/shard_map/ppermute | solution.py:14
  187.4 4.4 %collective-permute-start.5 = (f32[144,128]{1,0:T(8,128)S(1)}, f32[144,128]{1,0:T(8,128)S(1)}, u32[]{:S(2)}, u32[]{:S(2)}) collective-permute-start(f32[144,128]{1,0:T(8,128)S(1)} %add.207), channel_id=1, source_target_pairs={{0,8},{4,12},{8,0},{12,4},{16,24},{20,28},{24,16},{28,20},{1,9},{5... | collective-permute-start | bytes 221192 | tf_op jit(solution)/shard_map/ppermute | solution.py:14
  196.0 5.5 %collective-permute-start.6 = (f32[1,8,2048]{2,1,0:T(8,128)}, f32[1,8,2048]{2,1,0:T(8,128)}, u32[]{:S(2)}, u32[]{:S(2)}) collective-permute-start(f32[1,8,2048]{2,1,0:T(8,128)} %copy.65), channel_id=1, source_target_pairs={{0,16},{4,20},{8,24},{12,28},{16,0},{20,4},{24,8},{28,12},{1,17},{... | collective-permute-start | bytes 196616 | tf_op jit(solution)/shard_map/ppermute | solution.py:14
  203.0 11.2 %collective-permute-start.7 = (f32[1,8,1024]{1,2,0:T(8,128)S(1)}, f32[1,8,1024]{1,2,0:T(8,128)S(1)}, u32[]{:S(2)}, u32[]{:S(2)}) collective-permute-start(f32[1,8,1024]{1,2,0:T(8,128)S(1)} %slice_select_fusion.1), channel_id=1, source_target_pairs={{0,8},{4,12},{8,0},{12,4},{16,24},{20,28},{24,16},{28,20},{1,9},{5... | collective-permute-start | bytes 98312 | tf_op jit(solution)/shard_map/ppermute | solution.py:14
  214.4 6.4 %collective-permute-start.8 = (f32[1,8,512]{1,2,0:T(8,128)S(1)}, f32[1,8,512]{1,2,0:T(8,128)S(1)}, u32[]{:S(2)}, u32[]{:S(2)}) collective-permute-start(f32[1,8,512]{1,2,0:T(8,128)S(1)} %slice_select_fusion.2), channel_id=1, source_target_pairs={{0,4},{4,0},{8,12},{12,8},{16,20},{20,16},{24,28},{28,24},{1,5},{5... | collective-permute-start | bytes 49160 | tf_op jit(solution)/shard_map/ppermute | solution.py:14
  221.6 53.9 %all-reduce.11.cloned.1.call-start = ((), (), s32[]{:S(2)}) async-start(), calls=%async_computation.9 | async-start | bytes 147456 | tf_op jit(solution)/shard_map/psum | solution.py:42
  275.5 4.9 %collective-permute-start.9 = (f32[144,128]{1,0:T(8,128)}, f32[144,128]{1,0:T(8,128)S(1)}, u32[]{:S(2)}, u32[]{:S(2)}) collective-permute-start(f32[144,128]{1,0:T(8,128)} %all-reduce.11.cloned.1.call-done), channel_id=1, source_target_pairs={{0,4},{4,0},{8,12},{12,8},{16,20},{20,16},{24,28},{28,24},{1,5},{5... | collective-permute-start | bytes 221192 | tf_op jit(solution)/shard_map/ppermute | solution.py:14
  281.3 4.4 %collective-permute-start.10 = (f32[144,128]{1,0:T(8,128)S(1)}, f32[144,128]{1,0:T(8,128)S(1)}, u32[]{:S(2)}, u32[]{:S(2)}) collective-permute-start(f32[144,128]{1,0:T(8,128)S(1)} %add.219), channel_id=1, source_target_pairs={{0,8},{4,12},{8,0},{12,4},{16,24},{20,28},{24,16},{28,20},{1,9},{5... | collective-permute-start | bytes 221192 | tf_op jit(solution)/shard_map/ppermute | solution.py:14
  285.7 5.3 %collective-permute-start.11 = (f32[144,128]{1,0:T(8,128)S(1)}, f32[144,128]{1,0:T(8,128)S(1)}, u32[]{:S(2)}, u32[]{:S(2)}) collective-permute-start(f32[144,128]{1,0:T(8,128)S(1)} %add.220), channel_id=1, source_target_pairs={{0,16},{4,20},{8,24},{12,28},{16,0},{20,4},{24,8},{28,12},{1,17},{... | collective-permute-start | bytes 221192 | tf_op jit(solution)/shard_map/ppermute | solution.py:14
  304.6 4.6 %collective-permute-start.14 = (f32[8,128]{1,0:T(8,128)S(1)}, f32[8,128]{1,0:T(8,128)S(1)}, u32[]{:S(2)}, u32[]{:S(2)}) collective-permute-start(f32[8,128]{1,0:T(8,128)S(1)} %add.224), channel_id=1, source_target_pairs={{0,16},{4,20},{8,24},{12,28},{16,0},{20,4},{24,8},{28,12},{1,17},{... | collective-permute-start | bytes 12296 | tf_op jit(solution)/shard_map/ppermute | solution.py:14
  318.7 3.9 collective-permute-start.16
  322.6 5.2 %collective-permute-start.17 = (f32[1,8,2048]{2,1,0:T(8,128)S(1)}, f32[1,8,2048]{2,1,0:T(8,128)S(1)}, u32[]{:S(2)}, u32[]{:S(2)}) collective-permute-start(f32[1,8,2048]{2,1,0:T(8,128)S(1)} %maximum_select_fusion.2), channel_id=1, source_target_pairs={{0,16},{4,20},{8,24},{12,28},{16,0},{20,4},{24,8},{28,12},{1,17},{... | collective-permute-start | bytes 196616 | tf_op jit(solution)/shard_map/ppermute | solution.py:14
  351.5 3.9 collective-permute-start.20
  355.4 4.3 %collective-permute-start.21 = (f32[2,8,1024]{2,1,0:T(8,128)S(1)}, f32[2,8,1024]{2,1,0:T(8,128)S(1)}, u32[]{:S(2)}, u32[]{:S(2)}) collective-permute-start(f32[2,8,1024]{2,1,0:T(8,128)S(1)} %maximum_select_fusion.4), channel_id=1, source_target_pairs={{0,8},{4,12},{8,0},{12,4},{16,24},{20,28},{24,16},{28,20},{1,9},{5... | collective-permute-start | bytes 196616 | tf_op jit(solution)/shard_map/ppermute | solution.py:14
  (67 other events, 2687.7 us)
Sparse Core Ops, SparseCore 0:
  12.2 32.3 all-reduce.4
  52.9 21.4 reduce-scatter.3
  77.1 29.6 all-reduce.6
  128.0 21.1 reduce-scatter.5
  151.9 29.6 all-reduce.8
  221.7 20.8 reduce-scatter.7
  245.8 29.6 all-reduce.10
where the time goes:
time: 398 us; the launch traced here: 397 us
  waiting for transfers between devices  239 us (60%)
  starting transfers between devices  45.5 us (11%)
  blocking collectives  40.3 us (10%)
  matrix products  24 us (6%)
  other arithmetic  20.3 us (5%)
  between operations  15.1 us (4%)
  local copies, waits for them, and re-layouts  13.5 us (3%)
    psum x4, waiting for transfers between devices, paired_total(): summed = lax.psum(partial_value, 'grid')  115 us
    reduce_scatter x3, waiting for transfers between devices, group_extend(): return lax.psum_scatter(stack, 'grid', scatter_dimension=2, tiled=True)  62.6 us
    ppermute x24, waiting for transfers between devices, from_partner(): return lax.ppermute(value, axis, pairs)  60.9 us
    ppermute x24, starting transfers between devices, from_partner(): return lax.ppermute(value, axis, pairs)  45.2 us
    psum x4, blocking collectives, paired_total(): summed = lax.psum(partial_value, 'grid')  24 us
    all_gather x3, blocking collectives, group_fetch(): current = lax.all_gather(stack, 'grid', axis=2, tiled=True)  16.4 us
    dot_general x18, matrix products, mult(): jnp.dot(left, right, precision=HIGH_PRECISION, preferred_element_type=jnp...  8.73 us
  transfers between devices with their start and end apart: 31, of which 31 were waited for; matrix products, arithmetic and copies ran while one was open for 3% of the time, Pallas kernels for 0%

commit v1 on v0

--- a/solution.py
+++ b/solution.py
@@ -39,7 +39,8 @@
 
 
 def paired_total(partial_value, bits):
-    summed = lax.psum(partial_value, "grid")
+    blocks = lax.all_gather(partial_value, "grid", axis=0, tiled=False)
+    summed = blocks.sum(axis=0)
     for bit in range(bits):
         summed = summed + from_partner(summed, "leaf", bit)
     return summed

time: 398 us -> 289 us (0.73)
  waiting for transfers between devices: 239 us -> 122 us
  blocking collectives: 40.3 us -> 61.6 us
  other arithmetic: 20.3 us -> 12.2 us
    psum x4 -> x0, waiting for transfers between devices: 115 us -> none  [paired_total(): summed = lax.psum(partial_value, 'grid')]
    all_gather x0 -> x8, blocking collectives: none -> 45.8 us  [paired_total(): blocks = lax.all_gather(partial_value, 'grid', axis=0, tiled=False)]
    psum x4 -> x0, blocking collectives: 24 us -> none  [paired_total(): summed = lax.psum(partial_value, 'grid')]
  transfers between devices with their start and end apart: 31 -> 27, of which waited for: 31 -> 27; matrix products, arithmetic and copies ran while one was open for 3% -> 3% of each run, Pallas kernels for 0% -> 0%
where the time goes in v1:
time: 289 us; the launch traced here: 288 us
  waiting for transfers between devices  122 us (42%)
  blocking collectives  61.6 us (21%)
  starting transfers between devices  41.7 us (14%)
  matrix products  21.9 us (8%)
  between operations  14.7 us (5%)
  local copies, waits for them, and re-layouts  14.2 us (5%)
  other arithmetic  12.2 us (4%)
    ppermute x24, waiting for transfers between devices, from_partner(): return lax.ppermute(value, axis, pairs)  61.6 us
    reduce_scatter x3, waiting for transfers between devices, group_extend(): return lax.psum_scatter(stack, 'grid', scatter_dimension=2, tiled=True)  60 us
    all_gather x8, blocking collectives, paired_total(): blocks = lax.all_gather(partial_value, 'grid', axis=0, tiled=False)  45.8 us
    ppermute x24, starting transfers between devices, from_partner(): return lax.ppermute(value, axis, pairs)  41.6 us
    all_gather x3, blocking collectives, group_fetch(): current = lax.all_gather(stack, 'grid', axis=2, tiled=True)  15.8 us
    dot_general x18, matrix products, mult(): jnp.dot(left, right, precision=HIGH_PRECISION, preferred_element_type=jnp...  7.23 us
    dot_general x17, matrix products, outer(): lax.dot_general(left, right, (((1,), (1,)), ((), ())), precision=HIGH_PRE...  5.93 us
  transfers between devices with their start and end apart: 27, of which 27 were waited for; matrix products, arithmetic and copies ran while one was open for 3% of the time, Pallas kernels for 0%

profile of v1, /device:TPU:0, one launch (start us, length us, event | category | flops | bytes accessed | tf_op | source)
XLA Modules:
  0.0 287.9 jit_solution(18311446836549763083)
XLA Ops:
  12.7 7.4 %all-gather = f32[576,128]{1,0:T(8,128)S(1)} all-gather(f32[144,128]{1,0:T(8,128)S(1)} %pad_maximum_fusion), channel_id=2, replica_groups=mesh['leaf'=8,'grid'=4] {'grid'}, dimensions={0}, use_global_device_ids=true | all-gather | bytes 368640 | tf_op jit(solution)/shard_map/all_gather | solution.py:42
  30.9 20.1 %reduce-scatter.4.cloned.1.call-done = f32[2,8,128]{2,1,0:T(8,128)} async-done(((f32[2,8,512]{2,1,0:T(8,128)}), f32[2,8,128]{2,1,0:T(8,128)}) %reduce-scatter.4.cloned.1.call-update) | async-done | bytes 8208 | tf_op jit(solution)/shard_map/reduce_scatter | solution.py:66
  52.9 5.9 %all-gather.1 = f32[576,128]{1,0:T(8,128)S(1)} all-gather(f32[144,128]{1,0:T(8,128)S(1)} %pad_maximum_fusion.1), channel_id=3, replica_groups=mesh['leaf'=8,'grid'=4] {'grid'}, dimensions={0}, use_global_device_ids=true | all-gather | bytes 368640 | tf_op jit(solution)/shard_map/all_gather | solution.py:42
  71.3 2.8 collective-permute-done.2
  79.3 19.1 %reduce-scatter.6.cloned.1.call-done = f32[2,8,128]{2,1,0:T(8,128)} async-done(((f32[2,8,512]{2,1,0:T(8,128)}), f32[2,8,128]{2,1,0:T(8,128)}) %reduce-scatter.6.cloned.1.call-update) | async-done | bytes 8208 | tf_op jit(solution)/shard_map/reduce_scatter | solution.py:66
  100.3 5.9 %all-gather.2 = f32[576,128]{1,0:T(8,128)S(1)} all-gather(f32[144,128]{1,0:T(8,128)S(1)} %pad_maximum_fusion.2), channel_id=4, replica_groups=mesh['leaf'=8,'grid'=4] {'grid'}, dimensions={0}, use_global_device_ids=true | all-gather | bytes 368640 | tf_op jit(solution)/shard_map/all_gather | solution.py:42
  128.9 8.6 %collective-permute-done.7 = f32[1,8,1024]{1,2,0:T(8,128)S(1)} collective-permute-done((f32[1,8,1024]{1,2,0:T(8,128)S(1)}, f32[1,8,1024]{1,2,0:T(8,128)S(1)}, u32[]{:S(2)}, u32[]{:S(2)}) %collective-permute-start.7) | collective-permute-done | bytes 32800 | tf_op jit(solution)/shard_map/ppermute | solution.py:14
  139.4 4.8 %collective-permute-done.8 = f32[1,8,512]{1,2,0:T(8,128)S(1)} collective-permute-done((f32[1,8,512]{1,2,0:T(8,128)S(1)}, f32[1,8,512]{1,2,0:T(8,128)S(1)}, u32[]{:S(2)}, u32[]{:S(2)}) %collective-permute-start.8) | collective-permute-done | bytes 16416 | tf_op jit(solution)/shard_map/ppermute | solution.py:14
  145.1 20.8 %reduce-scatter.8.cloned.1.call-done = f32[1,8,128]{1,2,0:T(8,128)} async-done(((f32[1,8,512]{1,2,0:T(8,128)}), f32[1,8,128]{1,2,0:T(8,128)}) %reduce-scatter.8.cloned.1.call-update) | async-done | bytes 4112 | tf_op jit(solution)/shard_map/reduce_scatter | solution.py:66
  168.2 5.9 %all-gather.3 = f32[576,128]{1,0:T(8,128)S(1)} all-gather(f32[144,128]{1,0:T(8,128)S(1)} %pad_maximum_fusion.3), channel_id=5, replica_groups=mesh['leaf'=8,'grid'=4] {'grid'}, dimensions={0}, use_global_device_ids=true | all-gather | bytes 368640 | tf_op jit(solution)/shard_map/all_gather | solution.py:42
  175.7 3.0 %collective-permute-done.9 = f32[144,128]{1,0:T(8,128)S(1)} collective-permute-done((f32[144,128]{1,0:T(8,128)S(1)}, f32[144,128]{1,0:T(8,128)S(1)}, u32[]{:S(2)}, u32[]{:S(2)}) %collective-permute-start.9) | collective-permute-done | bytes 73760 | tf_op jit(solution)/shard_map/ppermute | solution.py:14
  180.3 2.8 collective-permute-done.10
  183.2 2.5 collective-permute-start.11
  185.8 2.8 collective-permute-done.11
  188.9 5.2 %all-gather.4 = f32[32,128]{1,0:T(8,128)S(1)} all-gather(f32[8,128]{1,0:T(8,128)S(1)} %fusion.123), channel_id=6, replica_groups=mesh['leaf'=8,'grid'=4] {'grid'}, dimensions={0}, use_global_device_ids=true | all-gather | bytes 20480 | tf_op jit(solution)/shard_map/all_gather | solution.py:42
  201.4 2.7 collective-permute-start.14
  206.0 5.4 %all-gather.5 = f32[8,512]{1,0:T(8,128)S(1)} all-gather(f32[8,128]{1,0:T(8,128)S(1)} %convolution_add_fusion.3), channel_id=7, replica_groups=mesh['leaf'=8,'grid'=4] {'grid'}, dimensions={1}, use_global_device_ids=true | all-gather | bytes 20480 | tf_op jit(solution)/shard_map/all_gather | solution.py:70
  219.1 2.7 collective-permute-start.17
  221.9 2.5 collective-permute-done.17
  225.9 5.2 %all-gather.6 = f32[64,128]{1,0:T(8,128)S(1)} all-gather(f32[16,128]{1,0:T(8,128)S(1)} %pad_maximum_fusion.6), channel_id=8, replica_groups=mesh['leaf'=8,'grid'=4] {'grid'}, dimensions={0}, use_global_device_ids=true | all-gather | bytes 40960 | tf_op jit(solution)/shard_map/all_gather | solution.py:42
  239.3 5.2 %all_gather.70 = f32[2,8,512]{2,1,0:T(8,128)S(1)} all-gather(f32[2,8,128]{2,1,0:T(8,128)S(1)} %pad_maximum_fusion.7), channel_id=1, replica_groups=mesh['leaf'=8,'grid'=4] {'grid'}, dimensions={2}, use_global_device_ids=true | all-gather | bytes 40960 | tf_op jit(solution)/shard_map/all_gather | solution.py:70
  254.3 5.2 %all-gather.7 = f32[64,128]{1,0:T(8,128)S(1)} all-gather(f32[16,128]{1,0:T(8,128)S(1)} %pad_maximum_fusion.8), channel_id=9, replica_groups=mesh['leaf'=8,'grid'=4] {'grid'}, dimensions={0}, use_global_device_ids=true | all-gather | bytes 40960 | tf_op jit(solution)/shard_map/all_gather | solution.py:42
  264.1 5.2 %all_gather.73 = f32[2,8,512]{2,1,0:T(8,128)S(1)} all-gather(f32[2,8,128]{2,1,0:T(8,128)S(1)} %pad_maximum_fusion.9), channel_id=1, replica_groups=mesh['leaf'=8,'grid'=4] {'grid'}, dimensions={2}, use_global_device_ids=true | all-gather | bytes 40960 | tf_op jit(solution)/shard_map/all_gather | solution.py:70
  274.7 5.2 %all-gather.8 = f32[64,128]{1,0:T(8,128)S(1)} all-gather(f32[16,128]{1,0:T(8,128)S(1)} %pad_maximum_fusion.10), channel_id=10, replica_groups=mesh['leaf'=8,'grid'=4] {'grid'}, dimensions={0}, use_global_device_ids=true | all-gather | bytes 40960 | tf_op jit(solution)/shard_map/all_gather | solution.py:42
  (312 shorter events, 116.5 us)
Async XLA Ops:
  7.2 43.8 %reduce-scatter.4.cloned.1.call-start = ((), (), s32[]{:S(2)}) async-start(), calls=%async_computation.3 | async-start | bytes 40960 | tf_op jit(solution)/shard_map/reduce_scatter | solution.py:66
  25.5 4.0 %collective-permute-start = (f32[2,8,512]{2,1,0:T(8,128)S(1)}, f32[2,8,512]{2,1,0:T(8,128)S(1)}, u32[]{:S(2)}, u32[]{:S(2)}) collective-permute-start(f32[2,8,512]{2,1,0:T(8,128)S(1)} %broadcast_select_fusion.1), channel_id=1, source_target_pairs={{0,4},{4,0},{8,12},{12,8},{16,20},{20,16},{24,28},{28,24},{1,5},{5... | collective-permute-start | bytes 98312 | tf_op jit(solution)/shard_map/ppermute | solution.py:14
  30.1 68.3 %reduce-scatter.6.cloned.1.call-start = ((), (), s32[]{:S(2)}) async-start(), calls=%async_computation.4 | async-start | bytes 40960 | tf_op jit(solution)/shard_map/reduce_scatter | solution.py:66
  58.8 4.6 %collective-permute-start.1 = (f32[144,128]{1,0:T(8,128)S(1)}, f32[144,128]{1,0:T(8,128)S(1)}, u32[]{:S(2)}, u32[]{:S(2)}) collective-permute-start(f32[144,128]{1,0:T(8,128)S(1)} %reduce_sum.73), channel_id=1, source_target_pairs={{0,4},{4,0},{8,12},{12,8},{16,20},{20,16},{24,28},{28,24},{1,5},{5... | collective-permute-start | bytes 221192 | tf_op jit(solution)/shard_map/ppermute | solution.py:14
  69.7 4.3 %collective-permute-start.2 = (f32[2,8,1024]{2,1,0:T(8,128)S(1)}, f32[2,8,1024]{2,1,0:T(8,128)S(1)}, u32[]{:S(2)}, u32[]{:S(2)}) collective-permute-start(f32[2,8,1024]{2,1,0:T(8,128)S(1)} %broadcast_select_fusion), channel_id=1, source_target_pairs={{0,8},{4,12},{8,0},{12,4},{16,24},{20,28},{24,16},{28,20},{1,9},{5... | collective-permute-start | bytes 196616 | tf_op jit(solution)/shard_map/ppermute | solution.py:14
  74.1 4.0 %collective-permute-start.3 = (f32[2,8,512]{2,1,0:T(8,128)S(1)}, f32[2,8,512]{2,1,0:T(8,128)S(1)}, u32[]{:S(2)}, u32[]{:S(2)}) collective-permute-start(f32[2,8,512]{2,1,0:T(8,128)S(1)} %slice_select_fusion.3), channel_id=1, source_target_pairs={{0,4},{4,0},{8,12},{12,8},{16,20},{20,16},{24,28},{28,24},{1,5},{5... | collective-permute-start | bytes 98312 | tf_op jit(solution)/shard_map/ppermute | solution.py:14
  78.7 87.1 %reduce-scatter.8.cloned.1.call-start = ((), (), s32[]{:S(2)}) async-start(), calls=%async_computation.5 | async-start | bytes 327680 | tf_op jit(solution)/shard_map/reduce_scatter | solution.py:66
  106.2 4.6 %collective-permute-start.4 = (f32[144,128]{1,0:T(8,128)S(1)}, f32[144,128]{1,0:T(8,128)S(1)}, u32[]{:S(2)}, u32[]{:S(2)}) collective-permute-start(f32[144,128]{1,0:T(8,128)S(1)} %reduce_sum.74), channel_id=1, source_target_pairs={{0,4},{4,0},{8,12},{12,8},{16,20},{20,16},{24,28},{28,24},{1,5},{5... | collective-permute-start | bytes 221192 | tf_op jit(solution)/shard_map/ppermute | solution.py:14
  110.8 4.4 %collective-permute-start.5 = (f32[144,128]{1,0:T(8,128)S(1)}, f32[144,128]{1,0:T(8,128)S(1)}, u32[]{:S(2)}, u32[]{:S(2)}) collective-permute-start(f32[144,128]{1,0:T(8,128)S(1)} %add.191), channel_id=1, source_target_pairs={{0,8},{4,12},{8,0},{12,4},{16,24},{20,28},{24,16},{28,20},{1,9},{5... | collective-permute-start | bytes 221192 | tf_op jit(solution)/shard_map/ppermute | solution.py:14
  119.4 5.5 %collective-permute-start.6 = (f32[1,8,2048]{2,1,0:T(8,128)}, f32[1,8,2048]{2,1,0:T(8,128)}, u32[]{:S(2)}, u32[]{:S(2)}) collective-permute-start(f32[1,8,2048]{2,1,0:T(8,128)} %copy.65), channel_id=1, source_target_pairs={{0,16},{4,20},{8,24},{12,28},{16,0},{20,4},{24,8},{28,12},{1,17},{... | collective-permute-start | bytes 196616 | tf_op jit(solution)/shard_map/ppermute | solution.py:14
  126.4 11.1 %collective-permute-start.7 = (f32[1,8,1024]{1,2,0:T(8,128)S(1)}, f32[1,8,1024]{1,2,0:T(8,128)S(1)}, u32[]{:S(2)}, u32[]{:S(2)}) collective-permute-start(f32[1,8,1024]{1,2,0:T(8,128)S(1)} %slice_select_fusion.1), channel_id=1, source_target_pairs={{0,8},{4,12},{8,0},{12,4},{16,24},{20,28},{24,16},{28,20},{1,9},{5... | collective-permute-start | bytes 98312 | tf_op jit(solution)/shard_map/ppermute | solution.py:14
  137.7 6.4 %collective-permute-start.8 = (f32[1,8,512]{1,2,0:T(8,128)S(1)}, f32[1,8,512]{1,2,0:T(8,128)S(1)}, u32[]{:S(2)}, u32[]{:S(2)}) collective-permute-start(f32[1,8,512]{1,2,0:T(8,128)S(1)} %slice_select_fusion.2), channel_id=1, source_target_pairs={{0,4},{4,0},{8,12},{12,8},{16,20},{20,16},{24,28},{28,24},{1,5},{5... | collective-permute-start | bytes 49160 | tf_op jit(solution)/shard_map/ppermute | solution.py:14
  174.1 4.6 %collective-permute-start.9 = (f32[144,128]{1,0:T(8,128)S(1)}, f32[144,128]{1,0:T(8,128)S(1)}, u32[]{:S(2)}, u32[]{:S(2)}) collective-permute-start(f32[144,128]{1,0:T(8,128)S(1)} %reduce_sum.75), channel_id=1, source_target_pairs={{0,4},{4,0},{8,12},{12,8},{16,20},{20,16},{24,28},{28,24},{1,5},{5... | collective-permute-start | bytes 221192 | tf_op jit(solution)/shard_map/ppermute | solution.py:14
  178.7 4.4 %collective-permute-start.10 = (f32[144,128]{1,0:T(8,128)S(1)}, f32[144,128]{1,0:T(8,128)S(1)}, u32[]{:S(2)}, u32[]{:S(2)}) collective-permute-start(f32[144,128]{1,0:T(8,128)S(1)} %add.203), channel_id=1, source_target_pairs={{0,8},{4,12},{8,0},{12,4},{16,24},{20,28},{24,16},{28,20},{1,9},{5... | collective-permute-start | bytes 221192 | tf_op jit(solution)/shard_map/ppermute | solution.py:14
  183.2 5.3 %collective-permute-start.11 = (f32[144,128]{1,0:T(8,128)S(1)}, f32[144,128]{1,0:T(8,128)S(1)}, u32[]{:S(2)}, u32[]{:S(2)}) collective-permute-start(f32[144,128]{1,0:T(8,128)S(1)} %add.204), channel_id=1, source_target_pairs={{0,16},{4,20},{8,24},{12,28},{16,0},{20,4},{24,8},{28,12},{1,17},{... | collective-permute-start | bytes 221192 | tf_op jit(solution)/shard_map/ppermute | solution.py:14
  201.4 4.5 %collective-permute-start.14 = (f32[8,128]{1,0:T(8,128)S(1)}, f32[8,128]{1,0:T(8,128)S(1)}, u32[]{:S(2)}, u32[]{:S(2)}) collective-permute-start(f32[8,128]{1,0:T(8,128)S(1)} %add.208), channel_id=1, source_target_pairs={{0,16},{4,20},{8,24},{12,28},{16,0},{20,4},{24,8},{28,12},{1,17},{... | collective-permute-start | bytes 12296 | tf_op jit(solution)/shard_map/ppermute | solution.py:14
  211.5 3.7 %collective-permute-start.15 = (f32[1,8,512]{2,1,0:T(8,128)S(1)}, f32[1,8,512]{2,1,0:T(8,128)S(1)}, u32[]{:S(2)}, u32[]{:S(2)}) collective-permute-start(f32[1,8,512]{2,1,0:T(8,128)S(1)} %bitcast.142), channel_id=1, source_target_pairs={{0,4},{4,0},{8,12},{12,8},{16,20},{20,16},{24,28},{28,24},{1,5},{5... | collective-permute-start | bytes 49160 | tf_op jit(solution)/shard_map/ppermute | solution.py:14
  215.2 3.9 %collective-permute-start.16 = (f32[1,8,1024]{2,1,0:T(8,128)S(1)}, f32[1,8,1024]{2,1,0:T(8,128)S(1)}, u32[]{:S(2)}, u32[]{:S(2)}) collective-permute-start(f32[1,8,1024]{2,1,0:T(8,128)S(1)} %maximum_select_fusion.6), channel_id=1, source_target_pairs={{0,8},{4,12},{8,0},{12,4},{16,24},{20,28},{24,16},{28,20},{1,9},{5... | collective-permute-start | bytes 98312 | tf_op jit(solution)/shard_map/ppermute | solution.py:14
  219.1 5.2 %collective-permute-start.17 = (f32[1,8,2048]{2,1,0:T(8,128)S(1)}, f32[1,8,2048]{2,1,0:T(8,128)S(1)}, u32[]{:S(2)}, u32[]{:S(2)}) collective-permute-start(f32[1,8,2048]{2,1,0:T(8,128)S(1)} %maximum_select_fusion.2), channel_id=1, source_target_pairs={{0,16},{4,20},{8,24},{12,28},{16,0},{20,4},{24,8},{28,12},{1,17},{... | collective-permute-start | bytes 196616 | tf_op jit(solution)/shard_map/ppermute | solution.py:14
  234.8 3.7 %collective-permute-start.19 = (f32[16,128]{1,0:T(8,128)S(1)}, f32[16,128]{1,0:T(8,128)S(1)}, u32[]{:S(2)}, u32[]{:S(2)}) collective-permute-start(f32[16,128]{1,0:T(8,128)S(1)} %add.211), channel_id=1, source_target_pairs={{0,8},{4,12},{8,0},{12,4},{16,24},{20,28},{24,16},{28,20},{1,9},{5... | collective-permute-start | bytes 24584 | tf_op jit(solution)/shard_map/ppermute | solution.py:14
  244.5 3.9 %collective-permute-start.20 = (f32[2,8,512]{2,1,0:T(8,128)S(1)}, f32[2,8,512]{2,1,0:T(8,128)S(1)}, u32[]{:S(2)}, u32[]{:S(2)}) collective-permute-start(f32[2,8,512]{2,1,0:T(8,128)S(1)} %all_gather.70), channel_id=1, source_target_pairs={{0,4},{4,0},{8,12},{12,8},{16,20},{20,16},{24,28},{28,24},{1,5},{5... | collective-permute-start | bytes 98312 | tf_op jit(solution)/shard_map/ppermute | solution.py:14
  248.4 4.3 %collective-permute-start.21 = (f32[2,8,1024]{2,1,0:T(8,128)S(1)}, f32[2,8,1024]{2,1,0:T(8,128)S(1)}, u32[]{:S(2)}, u32[]{:S(2)}) collective-permute-start(f32[2,8,1024]{2,1,0:T(8,128)S(1)} %maximum_select_fusion.4), channel_id=1, source_target_pairs={{0,8},{4,12},{8,0},{12,4},{16,24},{20,28},{24,16},{28,20},{1,9},{5... | collective-permute-start | bytes 196616 | tf_op jit(solution)/shard_map/ppermute | solution.py:14
  259.5 3.7 %collective-permute-start.22 = (f32[16,128]{1,0:T(8,128)S(1)}, f32[16,128]{1,0:T(8,128)S(1)}, u32[]{:S(2)}, u32[]{:S(2)}) collective-permute-start(f32[16,128]{1,0:T(8,128)S(1)} %reduce_sum.78), channel_id=1, source_target_pairs={{0,4},{4,0},{8,12},{12,8},{16,20},{20,16},{24,28},{28,24},{1,5},{5... | collective-permute-start | bytes 24584 | tf_op jit(solution)/shard_map/ppermute | solution.py:14
  269.3 3.9 %collective-permute-start.23 = (f32[2,8,512]{2,1,0:T(8,128)S(1)}, f32[2,8,512]{2,1,0:T(8,128)S(1)}, u32[]{:S(2)}, u32[]{:S(2)}) collective-permute-start(f32[2,8,512]{2,1,0:T(8,128)S(1)} %all_gather.73), channel_id=1, source_target_pairs={{0,4},{4,0},{8,12},{12,8},{16,20},{20,16},{24,28},{28,24},{1,5},{5... | collective-permute-start | bytes 98312 | tf_op jit(solution)/shard_map/ppermute | solution.py:14
  (67 other events, 1966.8 us)
Sparse Core Ops, SparseCore 0:
  30.3 20.6 reduce-scatter.3
  78.8 19.5 reduce-scatter.5
  145.0 20.7 reduce-scatter.7
